TPU v7x, 32 devices: a whole 2x2x4 slice. The times are simulated.
32 devices in a mesh: tm: 8 (over y, x, core), gy: 4 (over z).
Axes of the slice: x: 2, y: 2, z: 4, core: 2. Of those that a mesh axis runs over, the one named last changes fastest.
Arguments:
- initial_state: float32 [3, 64, 1024], P(None, 'gy'), may hold values from -4 to 4
- guessed_ends: float32 [8, 3, 64, 1024], P('tm', None, 'gy'), may hold values from -4 to 4
- velocity: float32 [8, 2, 64, 1024], P('tm', None, 'gy'), may hold values from -1 to 1
Outputs:
- corrected: float32 [8, 3, 64, 1024], P('tm', None, 'gy')
- relaxed: float32 [8, 3, 64, 1024], P('tm', None, 'gy')
All inputs are finite; a program needn't handle non-finite values.
Results may differ from a plain program's by a relative error of at most 0.00002.
Values sent between devices are 32-bit elements; how exact they have to be, the bound alone decides.
A program may use at most 64 MiB of HBM per device.

v0:
```python
import jax
import jax.numpy as jnp
from jax import lax
from jax.sharding import PartitionSpec as P

FINE = 4
GROUP = 4


diffusion = (0.05, 0.15, 0.4)
kappa_coupling = 0.1
time_step = 0.0125


def padded(block, sides, width):
    for axis, dim in sides:
        count = lax.axis_size(axis)
        forward = [(i, i + 1) for i in range(count - 1)]
        backward = [(target, source) for source, target in forward]
        low = lax.ppermute(
            lax.slice_in_dim(block, block.shape[dim] - width, None, axis=dim), axis, forward
        )
        high = lax.ppermute(lax.slice_in_dim(block, 0, width, axis=dim), axis, backward)
        block = jnp.concatenate([low, block, high], axis=dim)
    return block


def from_behind(block, axis, distance):
    devices = range(lax.axis_size(axis))
    route = [(i - distance, i) for i in devices if i - distance in devices]
    return lax.ppermute(block, axis, route)


def advance(extended, velocity, factor):
    center = extended[:, 1:-1]
    northern = extended[:, 2:]
    southern = extended[:, :-2]
    eastern = jnp.roll(center, -1, axis=2)
    western = jnp.roll(center, 1, axis=2)
    speed_across = velocity[0] + kappa_coupling * center[0]
    speed_along = velocity[1] + kappa_coupling * center[1]
    transport = jnp.maximum(speed_across, 0.0) * (center - western) + jnp.minimum(
        speed_across, 0.0
    ) * (eastern - center)
    transport = (
        transport
        + jnp.maximum(speed_along, 0.0) * (center - southern)
        + jnp.minimum(speed_along, 0.0) * (northern - center)
    )
    spread = northern + southern + eastern + western - 4.0 * center
    viscous = jnp.array(diffusion, jnp.float32)[:, None, None]
    return center + factor * (viscous * spread - transport)


def single(state, flow, factor):
    extended = padded(state, (("gy", 1),), 1)
    return advance(extended, flow, factor)


def from_left(state):
    return from_behind(state, "tm", 1)


def relayed(state, hops):
    for hop in range(hops):
        state = from_left(state)
    return state


def interval(state, flow, top_row, total_rows):
    extended = padded(jnp.concatenate([state, flow], axis=0), (("gy", 1),), FINE)
    height = state.shape[1]
    field = extended[:3]
    speeds = extended[3:]
    for section in range(FINE):
        kept = height + 2 * (FINE - section - 1)
        field = advance(field, speeds[:, section + 1 : section + 1 + kept], time_step)
        global_rows = top_row - (FINE - section - 1) + jnp.arange(kept)
        inside = (global_rows >= 0) & (global_rows < total_rows)
        field = jnp.where(inside[None, :, None], field, 0.0)
    return field


def per_device(initial_state, guessed_ends, velocity):
    state_here = guessed_ends[0]
    flow = velocity[0]
    groups = lax.axis_size("tm") // GROUP
    index_here = lax.axis_index("tm")
    position = index_here % GROUP
    cluster = index_here // GROUP
    height = initial_state.shape[1]
    top_row = lax.axis_index("gy") * height
    total_rows = height * lax.axis_size("gy")
    level_one = FINE * time_step
    coarsest = FINE * GROUP * time_step
    begin_state = jnp.where(index_here == 0, initial_state, from_left(state_here))
    fine_end = interval(begin_state, flow, top_row, total_rows)
    coarse_begin = single(begin_state, flow, level_one)
    sources = fine_end - coarse_begin
    current = coarse_begin + sources
    for k in range(1, GROUP):
        candidate = single(from_left(current), flow, level_one) + sources
        current = jnp.where(position == k, candidate, current)
    earlier = relayed(begin_state, GROUP - 1)
    forcing = current - single(earlier, flow, coarsest)

    def chain_step(j, state):
        candidate = single(relayed(state, GROUP), flow, coarsest) + forcing
        return jnp.where(cluster == j, candidate, state)

    settled = lax.fori_loop(1, groups, chain_step, single(initial_state, flow, coarsest) + forcing)
    previous = jnp.where(cluster == 0, initial_state, from_left(settled))
    current = single(previous, flow, level_one) + sources
    for k in range(1, GROUP - 1):
        candidate = single(from_left(current), flow, level_one) + sources
        current = jnp.where(position == k, candidate, current)
    corrected = jnp.where(position == GROUP - 1, settled, current)
    final_begin = jnp.where(index_here == 0, initial_state, from_left(corrected))
    relaxed = interval(final_begin, flow, top_row, total_rows)
    return (corrected[None], relaxed[None])


def solution(mesh):
    placed = (P(None, "gy", None), P("tm", None, "gy", None), P("tm", None, "gy", None))
    return jax.shard_map(
        per_device,
        mesh=mesh,
        in_specs=placed,
        out_specs=(P("tm", None, "gy", None), P("tm", None, "gy", None)),
        check_vma=False,
    )
```

profile of v0, /device:TPU:20, one launch (start us, length us, event | category | flops | bytes accessed | tf_op | source)
XLA Modules:
  0.0 184.0 jit_solution(11635460190636061386)
XLA Ops:
  3.5 2.4 %collective-permute-start = (f32[3,1,1024]{2,1,0:T(1,128)S(1)}, f32[3,1,1024]{2,1,0:T(1,128)S(1)}, u32[]{:S(2)}, u32[]{:S(2)}) collective-permute-start(f32[3,1,1024]{2,1,0:T(1,128)S(1)} %get-tuple-element.193), channel_id=1, source_target_pairs={{1,0},{2,1},{3,2},{5,4},{6,5},{7,6},{9,8},{10,9},{11,10},{13,12},{... | collective-permute-start | bytes 36872 | tf_op jit(solution)/shard_map/ppermute | solution.py:23
  5.9 3.5 %collective-permute-start.1 = (f32[3,1,1024]{2,1,0:T(1,128)S(1)}, f32[3,1,1024]{2,1,0:T(1,128)S(1)}, u32[]{:S(2)}, u32[]{:S(2)}) collective-permute-start(f32[3,1,1024]{2,1,0:T(1,128)S(1)} %get-tuple-element.194), channel_id=1, source_target_pairs={{0,1},{1,2},{2,3},{4,5},{5,6},{6,7},{8,9},{9,10},{10,11},{12,13},{... | collective-permute-start | bytes 36872 | tf_op jit(solution)/shard_map/ppermute | solution.py:20
  10.5 2.7 %collective-permute-start.5 = (f32[5,4,1024]{2,1,0:T(4,128)S(1)}, f32[5,4,1024]{2,1,0:T(4,128)S(1)}, u32[]{:S(2)}, u32[]{:S(2)}) collective-permute-start(f32[5,4,1024]{2,1,0:T(4,128)S(1)} %get-tuple-element.97), channel_id=1, source_target_pairs={{0,1},{1,2},{2,3},{4,5},{5,6},{6,7},{8,9},{9,10},{10,11},{12,13},{... | collective-permute-start | bytes 245768 | tf_op jit(solution)/shard_map/ppermute | solution.py:20
  13.2 3.1 %collective-permute-start.6 = (f32[5,4,1024]{2,1,0:T(4,128)S(1)}, f32[5,4,1024]{2,1,0:T(4,128)S(1)}, u32[]{:S(2)}, u32[]{:S(2)}) collective-permute-start(f32[5,4,1024]{2,1,0:T(4,128)S(1)} %get-tuple-element.98), channel_id=1, source_target_pairs={{1,0},{2,1},{3,2},{5,4},{6,5},{7,6},{9,8},{10,9},{11,10},{13,12},{... | collective-permute-start | bytes 245768 | tf_op jit(solution)/shard_map/ppermute | solution.py:23
  16.4 2.4 %collective-permute-start.16 = (f32[3,16,1024]{2,1,0:T(8,128)S(1)}, f32[3,16,1024]{2,1,0:T(8,128)S(1)}, u32[]{:S(2)}, u32[]{:S(2)}) collective-permute-start(f32[3,16,1024]{2,1,0:T(8,128)S(1)} %broadcast_select_fusion.2), channel_id=1, source_target_pairs={{0,4},{4,8},{8,12},{12,16},{16,20},{20,24},{24,28},{1,5},{5,9},{9,... | collective-permute-start | bytes 589832 | tf_op jit(solution)/shard_map/ppermute | solution.py:31
  18.8 2.4 %collective-permute-start.3 = (f32[3,1,1024]{2,1,0:T(1,128)S(1)}, f32[3,1,1024]{2,1,0:T(1,128)S(1)}, u32[]{:S(2)}, u32[]{:S(2)}) collective-permute-start(f32[3,1,1024]{2,1,0:T(1,128)S(1)} %get-tuple-element.181), channel_id=1, source_target_pairs={{1,0},{2,1},{3,2},{5,4},{6,5},{7,6},{9,8},{10,9},{11,10},{13,12},{... | collective-permute-start | bytes 36872 | tf_op jit(solution)/shard_map/ppermute | solution.py:23
  21.2 3.5 %collective-permute-start.4 = (f32[3,1,1024]{2,1,0:T(1,128)S(1)}, f32[3,1,1024]{2,1,0:T(1,128)S(1)}, u32[]{:S(2)}, u32[]{:S(2)}) collective-permute-start(f32[3,1,1024]{2,1,0:T(1,128)S(1)} %get-tuple-element.182), channel_id=1, source_target_pairs={{0,1},{1,2},{2,3},{4,5},{5,6},{6,7},{8,9},{9,10},{10,11},{12,13},{... | collective-permute-start | bytes 36872 | tf_op jit(solution)/shard_map/ppermute | solution.py:20
  27.9 2.5 %collective-permute-start.7 = (f32[3,16,1024]{2,1,0:T(8,128)S(1)}, f32[3,16,1024]{2,1,0:T(8,128)S(1)}, u32[]{:S(2)}, u32[]{:S(2)}) collective-permute-start(f32[3,16,1024]{2,1,0:T(8,128)S(1)} %get-tuple-element.18), channel_id=1, source_target_pairs={{0,4},{4,8},{8,12},{12,16},{16,20},{20,24},{24,28},{1,5},{5,9},{9,... | collective-permute-start | bytes 589832 | tf_op jit(solution)/shard_map/ppermute | solution.py:31
  30.6 2.5 %collective-permute-start.17 = (f32[3,16,1024]{2,1,0:T(8,128)S(1)}, f32[3,16,1024]{2,1,0:T(8,128)S(1)}, u32[]{:S(2)}, u32[]{:S(2)}) collective-permute-start(f32[3,16,1024]{2,1,0:T(8,128)S(1)} %collective-permute-done.16), channel_id=1, source_target_pairs={{0,4},{4,8},{8,12},{12,16},{16,20},{20,24},{24,28},{1,5},{5,9},{9,... | collective-permute-start | bytes 589832 | tf_op jit(solution)/shard_map/ppermute | solution.py:31
  33.1 2.8 %collective-permute-done.7 = f32[3,16,1024]{2,1,0:T(8,128)S(1)} collective-permute-done((f32[3,16,1024]{2,1,0:T(8,128)S(1)}, f32[3,16,1024]{2,1,0:T(8,128)S(1)}, u32[]{:S(2)}, u32[]{:S(2)}) %collective-permute-start.7) | collective-permute-done | bytes 196640 | tf_op jit(solution)/shard_map/ppermute | solution.py:31
  35.9 2.4 %collective-permute-start.8 = (f32[3,1,1024]{2,1,0:T(1,128)S(1)}, f32[3,1,1024]{2,1,0:T(1,128)S(1)}, u32[]{:S(2)}, u32[]{:S(2)}) collective-permute-start(f32[3,1,1024]{2,1,0:T(1,128)S(1)} %get-tuple-element.175), channel_id=1, source_target_pairs={{1,0},{2,1},{3,2},{5,4},{6,5},{7,6},{9,8},{10,9},{11,10},{13,12},{... | collective-permute-start | bytes 36872 | tf_op jit(solution)/shard_map/ppermute | solution.py:23
  38.2 3.5 %collective-permute-start.9 = (f32[3,1,1024]{2,1,0:T(1,128)S(1)}, f32[3,1,1024]{2,1,0:T(1,128)S(1)}, u32[]{:S(2)}, u32[]{:S(2)}) collective-permute-start(f32[3,1,1024]{2,1,0:T(1,128)S(1)} %get-tuple-element.176), channel_id=1, source_target_pairs={{0,1},{1,2},{2,3},{4,5},{5,6},{6,7},{8,9},{9,10},{10,11},{12,13},{... | collective-permute-start | bytes 36872 | tf_op jit(solution)/shard_map/ppermute | solution.py:20
  46.1 2.1 %collective-permute-start.18 = (f32[3,16,1024]{2,1,0:T(8,128)S(1)}, f32[3,16,1024]{2,1,0:T(8,128)S(1)}, u32[]{:S(2)}, u32[]{:S(2)}) collective-permute-start(f32[3,16,1024]{2,1,0:T(8,128)S(1)} %collective-permute-done.17), channel_id=1, source_target_pairs={{0,4},{4,8},{8,12},{12,16},{16,20},{20,24},{24,28},{1,5},{5,9},{9,... | collective-permute-start | bytes 589832 | tf_op jit(solution)/shard_map/ppermute | solution.py:31
  48.2 3.7 %collective-permute-done.10 = f32[3,16,1024]{2,1,0:T(8,128)S(1)} collective-permute-done((f32[3,16,1024]{2,1,0:T(8,128)S(1)}, f32[3,16,1024]{2,1,0:T(8,128)S(1)}, u32[]{:S(2)}, u32[]{:S(2)}) %collective-permute-start.10) | collective-permute-done | bytes 196640 | tf_op jit(solution)/shard_map/ppermute | solution.py:31
  52.0 2.1 %collective-permute-start.11 = (f32[3,1,1024]{2,1,0:T(1,128)S(1)}, f32[3,1,1024]{2,1,0:T(1,128)S(1)}, u32[]{:S(2)}, u32[]{:S(2)}) collective-permute-start(f32[3,1,1024]{2,1,0:T(1,128)S(1)} %get-tuple-element.169), channel_id=1, source_target_pairs={{1,0},{2,1},{3,2},{5,4},{6,5},{7,6},{9,8},{10,9},{11,10},{13,12},{... | collective-permute-start | bytes 36872 | tf_op jit(solution)/shard_map/ppermute | solution.py:23
  54.1 3.7 %collective-permute-start.12 = (f32[3,1,1024]{2,1,0:T(1,128)S(1)}, f32[3,1,1024]{2,1,0:T(1,128)S(1)}, u32[]{:S(2)}, u32[]{:S(2)}) collective-permute-start(f32[3,1,1024]{2,1,0:T(1,128)S(1)} %get-tuple-element.170), channel_id=1, source_target_pairs={{0,1},{1,2},{2,3},{4,5},{5,6},{6,7},{8,9},{9,10},{10,11},{12,13},{... | collective-permute-start | bytes 36872 | tf_op jit(solution)/shard_map/ppermute | solution.py:20
  63.8 3.9 %collective-permute-start.20 = (f32[3,1,1024]{2,1,0:T(1,128)S(1)}, f32[3,1,1024]{2,1,0:T(1,128)S(1)}, u32[]{:S(2)}, u32[]{:S(2)}) collective-permute-start(f32[3,1,1024]{2,1,0:T(1,128)S(1)} %get-tuple-element.184), channel_id=1, source_target_pairs={{0,1},{1,2},{2,3},{4,5},{5,6},{6,7},{8,9},{9,10},{10,11},{12,13},{... | collective-permute-start | bytes 36872 | tf_op jit(solution)/shard_map/ppermute | solution.py:20
  70.1 3.9 %collective-permute-start.15 = (f32[3,1,1024]{2,1,0:T(1,128)S(1)}, f32[3,1,1024]{2,1,0:T(1,128)S(1)}, u32[]{:S(2)}, u32[]{:S(2)}) collective-permute-start(f32[3,1,1024]{2,1,0:T(1,128)S(1)} %get-tuple-element.160), channel_id=1, source_target_pairs={{0,1},{1,2},{2,3},{4,5},{5,6},{6,7},{8,9},{9,10},{10,11},{12,13},{... | collective-permute-start | bytes 36872 | tf_op jit(solution)/shard_map/ppermute | solution.py:20
  78.3 6.0 %collective-permute-done.21 = f32[3,16,1024]{2,1,0:T(8,128)S(1)} collective-permute-done((f32[3,16,1024]{2,1,0:T(8,128)S(1)}, f32[3,16,1024]{2,1,0:T(8,128)S(1)}, u32[]{:S(2)}, u32[]{:S(2)}) %collective-permute-start.21) | collective-permute-done | bytes 196640 | tf_op jit(solution)/shard_map/while/body/eval_jaxpr/ppermute | solution.py:31
  86.1 6.0 %collective-permute-done.22 = f32[3,16,1024]{2,1,0:T(8,128)S(1)} collective-permute-done((f32[3,16,1024]{2,1,0:T(8,128)S(1)}, f32[3,16,1024]{2,1,0:T(8,128)S(1)}, u32[]{:S(2)}, u32[]{:S(2)}) %collective-permute-start.22) | collective-permute-done | bytes 196640 | tf_op jit(solution)/shard_map/while/body/eval_jaxpr/ppermute | solution.py:31
  94.0 6.0 %collective-permute-done.23 = f32[3,16,1024]{2,1,0:T(8,128)S(1)} collective-permute-done((f32[3,16,1024]{2,1,0:T(8,128)S(1)}, f32[3,16,1024]{2,1,0:T(8,128)S(1)}, u32[]{:S(2)}, u32[]{:S(2)}) %collective-permute-start.23) | collective-permute-done | bytes 196640 | tf_op jit(solution)/shard_map/while/body/eval_jaxpr/ppermute | solution.py:31
  101.9 5.9 %collective-permute-done.24 = f32[3,16,1024]{2,1,0:T(8,128)S(1)} collective-permute-done((f32[3,16,1024]{2,1,0:T(8,128)S(1)}, f32[3,16,1024]{2,1,0:T(8,128)S(1)}, u32[]{:S(2)}, u32[]{:S(2)}) %collective-permute-start.24) | collective-permute-done | bytes 196640 | tf_op jit(solution)/shard_map/while/body/eval_jaxpr/ppermute | solution.py:31
  109.8 3.9 %collective-permute-start.26 = (f32[3,1,1024]{2,1,0:T(1,128)S(1)}, f32[3,1,1024]{2,1,0:T(1,128)S(1)}, u32[]{:S(2)}, u32[]{:S(2)}) collective-permute-start(f32[3,1,1024]{2,1,0:T(1,128)S(1)} %get-tuple-element.158), channel_id=1, source_target_pairs={{0,1},{1,2},{2,3},{4,5},{5,6},{6,7},{8,9},{9,10},{10,11},{12,13},{... | collective-permute-start | bytes 36872 | tf_op jit(solution)/shard_map/while/body/eval_jaxpr/ppermute | solution.py:20
  117.6 6.0 %collective-permute-done.27 = f32[3,16,1024]{2,1,0:T(8,128)S(1)} collective-permute-done((f32[3,16,1024]{2,1,0:T(8,128)S(1)}, f32[3,16,1024]{2,1,0:T(8,128)S(1)}, u32[]{:S(2)}, u32[]{:S(2)}) %collective-permute-start.27) | collective-permute-done | bytes 196640 | tf_op jit(solution)/shard_map/ppermute | solution.py:31
  125.6 3.9 %collective-permute-start.29 = (f32[3,1,1024]{2,1,0:T(1,128)S(1)}, f32[3,1,1024]{2,1,0:T(1,128)S(1)}, u32[]{:S(2)}, u32[]{:S(2)}) collective-permute-start(f32[3,1,1024]{2,1,0:T(1,128)S(1)} %get-tuple-element.152), channel_id=1, source_target_pairs={{0,1},{1,2},{2,3},{4,5},{5,6},{6,7},{8,9},{9,10},{10,11},{12,13},{... | collective-permute-start | bytes 36872 | tf_op jit(solution)/shard_map/ppermute | solution.py:20
  133.4 6.0 %collective-permute-done.30 = f32[3,16,1024]{2,1,0:T(8,128)S(1)} collective-permute-done((f32[3,16,1024]{2,1,0:T(8,128)S(1)}, f32[3,16,1024]{2,1,0:T(8,128)S(1)}, u32[]{:S(2)}, u32[]{:S(2)}) %collective-permute-start.30) | collective-permute-done | bytes 196640 | tf_op jit(solution)/shard_map/ppermute | solution.py:31
  141.3 3.9 %collective-permute-start.32 = (f32[3,1,1024]{2,1,0:T(1,128)S(1)}, f32[3,1,1024]{2,1,0:T(1,128)S(1)}, u32[]{:S(2)}, u32[]{:S(2)}) collective-permute-start(f32[3,1,1024]{2,1,0:T(1,128)S(1)} %get-tuple-element.146), channel_id=1, source_target_pairs={{0,1},{1,2},{2,3},{4,5},{5,6},{6,7},{8,9},{9,10},{10,11},{12,13},{... | collective-permute-start | bytes 36872 | tf_op jit(solution)/shard_map/ppermute | solution.py:20
  149.0 6.0 %collective-permute-done.33 = f32[3,16,1024]{2,1,0:T(8,128)S(1)} collective-permute-done((f32[3,16,1024]{2,1,0:T(8,128)S(1)}, f32[3,16,1024]{2,1,0:T(8,128)S(1)}, u32[]{:S(2)}, u32[]{:S(2)}) %collective-permute-start.33) | collective-permute-done | bytes 196640 | tf_op jit(solution)/shard_map/ppermute | solution.py:31
  157.0 3.9 %collective-permute-start.35 = (f32[3,1,1024]{2,1,0:T(1,128)S(1)}, f32[3,1,1024]{2,1,0:T(1,128)S(1)}, u32[]{:S(2)}, u32[]{:S(2)}) collective-permute-start(f32[3,1,1024]{2,1,0:T(1,128)S(1)} %get-tuple-element.140), channel_id=1, source_target_pairs={{0,1},{1,2},{2,3},{4,5},{5,6},{6,7},{8,9},{9,10},{10,11},{12,13},{... | collective-permute-start | bytes 36872 | tf_op jit(solution)/shard_map/ppermute | solution.py:20
  164.7 6.0 %collective-permute-done.36 = f32[3,16,1024]{2,1,0:T(8,128)S(1)} collective-permute-done((f32[3,16,1024]{2,1,0:T(8,128)S(1)}, f32[3,16,1024]{2,1,0:T(8,128)S(1)}, u32[]{:S(2)}, u32[]{:S(2)}) %collective-permute-start.36) | collective-permute-done | bytes 196640 | tf_op jit(solution)/shard_map/ppermute | solution.py:31
  170.8 3.9 %collective-permute-start.37 = (f32[5,4,1024]{2,1,0:T(4,128)S(1)}, f32[5,4,1024]{2,1,0:T(4,128)S(1)}, u32[]{:S(2)}, u32[]{:S(2)}) collective-permute-start(f32[5,4,1024]{2,1,0:T(4,128)S(1)} %get-tuple-element.67), channel_id=1, source_target_pairs={{0,1},{1,2},{2,3},{4,5},{5,6},{6,7},{8,9},{9,10},{10,11},{12,13},{... | collective-permute-start | bytes 245768 | tf_op jit(solution)/shard_map/ppermute | solution.py:20
  177.1 3.9 %collective-permute-done.38 = f32[5,4,1024]{2,1,0:T(4,128)S(1)} collective-permute-done((f32[5,4,1024]{2,1,0:T(4,128)S(1)}, f32[5,4,1024]{2,1,0:T(4,128)S(1)}, u32[]{:S(2)}, u32[]{:S(2)}) %collective-permute-start.38) | collective-permute-done | bytes 81952 | tf_op jit(solution)/shard_map/ppermute | solution.py:23
  (141 shorter events, 58.3 us)
Async XLA Ops:
  0.6 8.8 %collective-permute-start.2 = (f32[3,16,1024]{2,1,0:T(8,128)}, f32[3,16,1024]{2,1,0:T(8,128)S(1)}, u32[]{:S(2)}, u32[]{:S(2)}) collective-permute-start(f32[3,16,1024]{2,1,0:T(8,128)} %bitcast.276), channel_id=1, source_target_pairs={{0,4},{4,8},{8,12},{12,16},{16,20},{20,24},{24,28},{1,5},{5,9},{9,... | collective-permute-start | bytes 589832 | tf_op jit(solution)/shard_map/ppermute | solution.py:31
  3.5 66.6 %collective-permute-start = (f32[3,1,1024]{2,1,0:T(1,128)S(1)}, f32[3,1,1024]{2,1,0:T(1,128)S(1)}, u32[]{:S(2)}, u32[]{:S(2)}) collective-permute-start(f32[3,1,1024]{2,1,0:T(1,128)S(1)} %get-tuple-element.193), channel_id=1, source_target_pairs={{1,0},{2,1},{3,2},{5,4},{6,5},{7,6},{9,8},{10,9},{11,10},{13,12},{... | collective-permute-start | bytes 36872 | tf_op jit(solution)/shard_map/ppermute | solution.py:23
  5.9 68.2 %collective-permute-start.1 = (f32[3,1,1024]{2,1,0:T(1,128)S(1)}, f32[3,1,1024]{2,1,0:T(1,128)S(1)}, u32[]{:S(2)}, u32[]{:S(2)}) collective-permute-start(f32[3,1,1024]{2,1,0:T(1,128)S(1)} %get-tuple-element.194), channel_id=1, source_target_pairs={{0,1},{1,2},{2,3},{4,5},{5,6},{6,7},{8,9},{9,10},{10,11},{12,13},{... | collective-permute-start | bytes 36872 | tf_op jit(solution)/shard_map/ppermute | solution.py:20
  10.5 8.3 %collective-permute-start.5 = (f32[5,4,1024]{2,1,0:T(4,128)S(1)}, f32[5,4,1024]{2,1,0:T(4,128)S(1)}, u32[]{:S(2)}, u32[]{:S(2)}) collective-permute-start(f32[5,4,1024]{2,1,0:T(4,128)S(1)} %get-tuple-element.97), channel_id=1, source_target_pairs={{0,1},{1,2},{2,3},{4,5},{5,6},{6,7},{8,9},{9,10},{10,11},{12,13},{... | collective-permute-start | bytes 245768 | tf_op jit(solution)/shard_map/ppermute | solution.py:20
  13.2 8.0 %collective-permute-start.6 = (f32[5,4,1024]{2,1,0:T(4,128)S(1)}, f32[5,4,1024]{2,1,0:T(4,128)S(1)}, u32[]{:S(2)}, u32[]{:S(2)}) collective-permute-start(f32[5,4,1024]{2,1,0:T(4,128)S(1)} %get-tuple-element.98), channel_id=1, source_target_pairs={{1,0},{2,1},{3,2},{5,4},{6,5},{7,6},{9,8},{10,9},{11,10},{13,12},{... | collective-permute-start | bytes 245768 | tf_op jit(solution)/shard_map/ppermute | solution.py:23
  16.4 14.2 %collective-permute-start.16 = (f32[3,16,1024]{2,1,0:T(8,128)S(1)}, f32[3,16,1024]{2,1,0:T(8,128)S(1)}, u32[]{:S(2)}, u32[]{:S(2)}) collective-permute-start(f32[3,16,1024]{2,1,0:T(8,128)S(1)} %broadcast_select_fusion.2), channel_id=1, source_target_pairs={{0,4},{4,8},{8,12},{12,16},{16,20},{20,24},{24,28},{1,5},{5,9},{9,... | collective-permute-start | bytes 589832 | tf_op jit(solution)/shard_map/ppermute | solution.py:31
  18.8 8.7 %collective-permute-start.3 = (f32[3,1,1024]{2,1,0:T(1,128)S(1)}, f32[3,1,1024]{2,1,0:T(1,128)S(1)}, u32[]{:S(2)}, u32[]{:S(2)}) collective-permute-start(f32[3,1,1024]{2,1,0:T(1,128)S(1)} %get-tuple-element.181), channel_id=1, source_target_pairs={{1,0},{2,1},{3,2},{5,4},{6,5},{7,6},{9,8},{10,9},{11,10},{13,12},{... | collective-permute-start | bytes 36872 | tf_op jit(solution)/shard_map/ppermute | solution.py:23
  21.2 6.3 %collective-permute-start.4 = (f32[3,1,1024]{2,1,0:T(1,128)S(1)}, f32[3,1,1024]{2,1,0:T(1,128)S(1)}, u32[]{:S(2)}, u32[]{:S(2)}) collective-permute-start(f32[3,1,1024]{2,1,0:T(1,128)S(1)} %get-tuple-element.182), channel_id=1, source_target_pairs={{0,1},{1,2},{2,3},{4,5},{5,6},{6,7},{8,9},{9,10},{10,11},{12,13},{... | collective-permute-start | bytes 36872 | tf_op jit(solution)/shard_map/ppermute | solution.py:20
  27.9 7.9 %collective-permute-start.7 = (f32[3,16,1024]{2,1,0:T(8,128)S(1)}, f32[3,16,1024]{2,1,0:T(8,128)S(1)}, u32[]{:S(2)}, u32[]{:S(2)}) collective-permute-start(f32[3,16,1024]{2,1,0:T(8,128)S(1)} %get-tuple-element.18), channel_id=1, source_target_pairs={{0,4},{4,8},{8,12},{12,16},{16,20},{20,24},{24,28},{1,5},{5,9},{9,... | collective-permute-start | bytes 589832 | tf_op jit(solution)/shard_map/ppermute | solution.py:31
  30.6 15.5 %collective-permute-start.17 = (f32[3,16,1024]{2,1,0:T(8,128)S(1)}, f32[3,16,1024]{2,1,0:T(8,128)S(1)}, u32[]{:S(2)}, u32[]{:S(2)}) collective-permute-start(f32[3,16,1024]{2,1,0:T(8,128)S(1)} %collective-permute-done.16), channel_id=1, source_target_pairs={{0,4},{4,8},{8,12},{12,16},{16,20},{20,24},{24,28},{1,5},{5,9},{9,... | collective-permute-start | bytes 589832 | tf_op jit(solution)/shard_map/ppermute | solution.py:31
  35.9 6.1 %collective-permute-start.8 = (f32[3,1,1024]{2,1,0:T(1,128)S(1)}, f32[3,1,1024]{2,1,0:T(1,128)S(1)}, u32[]{:S(2)}, u32[]{:S(2)}) collective-permute-start(f32[3,1,1024]{2,1,0:T(1,128)S(1)} %get-tuple-element.175), channel_id=1, source_target_pairs={{1,0},{2,1},{3,2},{5,4},{6,5},{7,6},{9,8},{10,9},{11,10},{13,12},{... | collective-permute-start | bytes 36872 | tf_op jit(solution)/shard_map/ppermute | solution.py:23
  44.1 7.9 %collective-permute-start.10 = (f32[3,16,1024]{2,1,0:T(8,128)S(1)}, f32[3,16,1024]{2,1,0:T(8,128)S(1)}, u32[]{:S(2)}, u32[]{:S(2)}) collective-permute-start(f32[3,16,1024]{2,1,0:T(8,128)S(1)} %fusion.124), channel_id=1, source_target_pairs={{0,4},{4,8},{8,12},{12,16},{16,20},{20,24},{24,28},{1,5},{5,9},{9,... | collective-permute-start | bytes 589832 | tf_op jit(solution)/shard_map/ppermute | solution.py:31
  46.1 15.8 %collective-permute-start.18 = (f32[3,16,1024]{2,1,0:T(8,128)S(1)}, f32[3,16,1024]{2,1,0:T(8,128)S(1)}, u32[]{:S(2)}, u32[]{:S(2)}) collective-permute-start(f32[3,16,1024]{2,1,0:T(8,128)S(1)} %collective-permute-done.17), channel_id=1, source_target_pairs={{0,4},{4,8},{8,12},{12,16},{16,20},{20,24},{24,28},{1,5},{5,9},{9,... | collective-permute-start | bytes 589832 | tf_op jit(solution)/shard_map/ppermute | solution.py:31
  52.0 6.1 %collective-permute-start.11 = (f32[3,1,1024]{2,1,0:T(1,128)S(1)}, f32[3,1,1024]{2,1,0:T(1,128)S(1)}, u32[]{:S(2)}, u32[]{:S(2)}) collective-permute-start(f32[3,1,1024]{2,1,0:T(1,128)S(1)} %get-tuple-element.169), channel_id=1, source_target_pairs={{1,0},{2,1},{3,2},{5,4},{6,5},{7,6},{9,8},{10,9},{11,10},{13,12},{... | collective-permute-start | bytes 36872 | tf_op jit(solution)/shard_map/ppermute | solution.py:23
  59.9 8.0 %collective-permute-start.13 = (f32[3,16,1024]{2,1,0:T(8,128)S(1)}, f32[3,16,1024]{2,1,0:T(8,128)S(1)}, u32[]{:S(2)}, u32[]{:S(2)}) collective-permute-start(f32[3,16,1024]{2,1,0:T(8,128)S(1)} %fusion.108), channel_id=1, source_target_pairs={{0,4},{4,8},{8,12},{12,16},{16,20},{20,24},{24,28},{1,5},{5,9},{9,... | collective-permute-start | bytes 589832 | tf_op jit(solution)/shard_map/ppermute | solution.py:31
  61.9 12.2 %collective-permute-start.19 = (f32[3,1,1024]{2,1,0:T(1,128)S(1)}, f32[3,1,1024]{2,1,0:T(1,128)S(1)}, u32[]{:S(2)}, u32[]{:S(2)}) collective-permute-start(f32[3,1,1024]{2,1,0:T(1,128)S(1)} %get-tuple-element.183), channel_id=1, source_target_pairs={{1,0},{2,1},{3,2},{5,4},{6,5},{7,6},{9,8},{10,9},{11,10},{13,12},{... | collective-permute-start | bytes 36872 | tf_op jit(solution)/shard_map/ppermute | solution.py:23
  63.8 10.3 %collective-permute-start.20 = (f32[3,1,1024]{2,1,0:T(1,128)S(1)}, f32[3,1,1024]{2,1,0:T(1,128)S(1)}, u32[]{:S(2)}, u32[]{:S(2)}) collective-permute-start(f32[3,1,1024]{2,1,0:T(1,128)S(1)} %get-tuple-element.184), channel_id=1, source_target_pairs={{0,1},{1,2},{2,3},{4,5},{5,6},{6,7},{8,9},{9,10},{10,11},{12,13},{... | collective-permute-start | bytes 36872 | tf_op jit(solution)/shard_map/ppermute | solution.py:20
  68.0 6.1 %collective-permute-start.14 = (f32[3,1,1024]{2,1,0:T(1,128)S(1)}, f32[3,1,1024]{2,1,0:T(1,128)S(1)}, u32[]{:S(2)}, u32[]{:S(2)}) collective-permute-start(f32[3,1,1024]{2,1,0:T(1,128)S(1)} %get-tuple-element.159), channel_id=1, source_target_pairs={{1,0},{2,1},{3,2},{5,4},{6,5},{7,6},{9,8},{10,9},{11,10},{13,12},{... | collective-permute-start | bytes 36872 | tf_op jit(solution)/shard_map/ppermute | solution.py:23
  76.3 7.9 %collective-permute-start.21 = (f32[3,16,1024]{2,1,0:T(8,128)S(1)}, f32[3,16,1024]{2,1,0:T(8,128)S(1)}, u32[]{:S(2)}, u32[]{:S(2)}) collective-permute-start(f32[3,16,1024]{2,1,0:T(8,128)S(1)} %get-tuple-element.16), channel_id=1, source_target_pairs={{0,4},{4,8},{8,12},{12,16},{16,20},{20,24},{24,28},{1,5},{5,9},{9,... | collective-permute-start | bytes 589832 | tf_op jit(solution)/shard_map/while/body/eval_jaxpr/ppermute | solution.py:31
  84.2 7.9 %collective-permute-start.22 = (f32[3,16,1024]{2,1,0:T(8,128)S(1)}, f32[3,16,1024]{2,1,0:T(8,128)S(1)}, u32[]{:S(2)}, u32[]{:S(2)}) collective-permute-start(f32[3,16,1024]{2,1,0:T(8,128)S(1)} %collective-permute-done.21), channel_id=1, source_target_pairs={{0,4},{4,8},{8,12},{12,16},{16,20},{20,24},{24,28},{1,5},{5,9},{9,... | collective-permute-start | bytes 589832 | tf_op jit(solution)/shard_map/while/body/eval_jaxpr/ppermute | solution.py:31
  92.1 7.9 %collective-permute-start.23 = (f32[3,16,1024]{2,1,0:T(8,128)S(1)}, f32[3,16,1024]{2,1,0:T(8,128)S(1)}, u32[]{:S(2)}, u32[]{:S(2)}) collective-permute-start(f32[3,16,1024]{2,1,0:T(8,128)S(1)} %collective-permute-done.22), channel_id=1, source_target_pairs={{0,4},{4,8},{8,12},{12,16},{16,20},{20,24},{24,28},{1,5},{5,9},{9,... | collective-permute-start | bytes 589832 | tf_op jit(solution)/shard_map/while/body/eval_jaxpr/ppermute | solution.py:31
  100.0 7.9 %collective-permute-start.24 = (f32[3,16,1024]{2,1,0:T(8,128)S(1)}, f32[3,16,1024]{2,1,0:T(8,128)S(1)}, u32[]{:S(2)}, u32[]{:S(2)}) collective-permute-start(f32[3,16,1024]{2,1,0:T(8,128)S(1)} %collective-permute-done.23), channel_id=1, source_target_pairs={{0,4},{4,8},{8,12},{12,16},{16,20},{20,24},{24,28},{1,5},{5,9},{9,... | collective-permute-start | bytes 589832 | tf_op jit(solution)/shard_map/while/body/eval_jaxpr/ppermute | solution.py:31
  107.9 6.1 %collective-permute-start.25 = (f32[3,1,1024]{2,1,0:T(1,128)S(1)}, f32[3,1,1024]{2,1,0:T(1,128)S(1)}, u32[]{:S(2)}, u32[]{:S(2)}) collective-permute-start(f32[3,1,1024]{2,1,0:T(1,128)S(1)} %get-tuple-element.157), channel_id=1, source_target_pairs={{1,0},{2,1},{3,2},{5,4},{6,5},{7,6},{9,8},{10,9},{11,10},{13,12},{... | collective-permute-start | bytes 36872 | tf_op jit(solution)/shard_map/while/body/eval_jaxpr/ppermute | solution.py:23
  115.6 7.9 %collective-permute-start.27 = (f32[3,16,1024]{2,1,0:T(8,128)S(1)}, f32[3,16,1024]{2,1,0:T(8,128)S(1)}, u32[]{:S(2)}, u32[]{:S(2)}) collective-permute-start(f32[3,16,1024]{2,1,0:T(8,128)S(1)} %fusion.61), channel_id=1, source_target_pairs={{0,4},{4,8},{8,12},{12,16},{16,20},{20,24},{24,28},{1,5},{5,9},{9,... | collective-permute-start | bytes 589832 | tf_op jit(solution)/shard_map/ppermute | solution.py:31
  123.7 5.9 %collective-permute-start.28 = (f32[3,1,1024]{2,1,0:T(1,128)S(1)}, f32[3,1,1024]{2,1,0:T(1,128)S(1)}, u32[]{:S(2)}, u32[]{:S(2)}) collective-permute-start(f32[3,1,1024]{2,1,0:T(1,128)S(1)} %get-tuple-element.151), channel_id=1, source_target_pairs={{1,0},{2,1},{3,2},{5,4},{6,5},{7,6},{9,8},{10,9},{11,10},{13,12},{... | collective-permute-start | bytes 36872 | tf_op jit(solution)/shard_map/ppermute | solution.py:23
  131.5 7.9 %collective-permute-start.30 = (f32[3,16,1024]{2,1,0:T(8,128)S(1)}, f32[3,16,1024]{2,1,0:T(8,128)S(1)}, u32[]{:S(2)}, u32[]{:S(2)}) collective-permute-start(f32[3,16,1024]{2,1,0:T(8,128)S(1)} %fusion.45), channel_id=1, source_target_pairs={{0,4},{4,8},{8,12},{12,16},{16,20},{20,24},{24,28},{1,5},{5,9},{9,... | collective-permute-start | bytes 589832 | tf_op jit(solution)/shard_map/ppermute | solution.py:31
  139.4 6.1 %collective-permute-start.31 = (f32[3,1,1024]{2,1,0:T(1,128)S(1)}, f32[3,1,1024]{2,1,0:T(1,128)S(1)}, u32[]{:S(2)}, u32[]{:S(2)}) collective-permute-start(f32[3,1,1024]{2,1,0:T(1,128)S(1)} %get-tuple-element.145), channel_id=1, source_target_pairs={{1,0},{2,1},{3,2},{5,4},{6,5},{7,6},{9,8},{10,9},{11,10},{13,12},{... | collective-permute-start | bytes 36872 | tf_op jit(solution)/shard_map/ppermute | solution.py:23
  147.1 7.9 %collective-permute-start.33 = (f32[3,16,1024]{2,1,0:T(8,128)S(1)}, f32[3,16,1024]{2,1,0:T(8,128)S(1)}, u32[]{:S(2)}, u32[]{:S(2)}) collective-permute-start(f32[3,16,1024]{2,1,0:T(8,128)S(1)} %fusion.30), channel_id=1, source_target_pairs={{0,4},{4,8},{8,12},{12,16},{16,20},{20,24},{24,28},{1,5},{5,9},{9,... | collective-permute-start | bytes 589832 | tf_op jit(solution)/shard_map/ppermute | solution.py:31
  155.0 6.1 %collective-permute-start.34 = (f32[3,1,1024]{2,1,0:T(1,128)S(1)}, f32[3,1,1024]{2,1,0:T(1,128)S(1)}, u32[]{:S(2)}, u32[]{:S(2)}) collective-permute-start(f32[3,1,1024]{2,1,0:T(1,128)S(1)} %get-tuple-element.139), channel_id=1, source_target_pairs={{1,0},{2,1},{3,2},{5,4},{6,5},{7,6},{9,8},{10,9},{11,10},{13,12},{... | collective-permute-start | bytes 36872 | tf_op jit(solution)/shard_map/ppermute | solution.py:23
  162.8 7.9 %collective-permute-start.36 = (f32[3,16,1024]{2,1,0:T(8,128)S(1)}, f32[3,16,1024]{2,1,0:T(8,128)S(1)}, u32[]{:S(2)}, u32[]{:S(2)}) collective-permute-start(f32[3,16,1024]{2,1,0:T(8,128)S(1)} %fusion.14), channel_id=1, source_target_pairs={{0,4},{4,8},{8,12},{12,16},{16,20},{20,24},{24,28},{1,5},{5,9},{9,... | collective-permute-start | bytes 589832 | tf_op jit(solution)/shard_map/ppermute | solution.py:31
  170.8 6.3 %collective-permute-start.37 = (f32[5,4,1024]{2,1,0:T(4,128)S(1)}, f32[5,4,1024]{2,1,0:T(4,128)S(1)}, u32[]{:S(2)}, u32[]{:S(2)}) collective-permute-start(f32[5,4,1024]{2,1,0:T(4,128)S(1)} %get-tuple-element.67), channel_id=1, source_target_pairs={{0,1},{1,2},{2,3},{4,5},{5,6},{6,7},{8,9},{9,10},{10,11},{12,13},{... | collective-permute-start | bytes 245768 | tf_op jit(solution)/shard_map/ppermute | solution.py:20
  174.7 6.3 %collective-permute-start.38 = (f32[5,4,1024]{2,1,0:T(4,128)S(1)}, f32[5,4,1024]{2,1,0:T(4,128)S(1)}, u32[]{:S(2)}, u32[]{:S(2)}) collective-permute-start(f32[5,4,1024]{2,1,0:T(4,128)S(1)} %get-tuple-element.68), channel_id=1, source_target_pairs={{1,0},{2,1},{3,2},{5,4},{6,5},{7,6},{9,8},{10,9},{11,10},{13,12},{... | collective-permute-start | bytes 245768 | tf_op jit(solution)/shard_map/ppermute | solution.py:23
  (11 other events, 51.6 us)
where the time goes:
time: 185 us; the launch traced here: 184 us
  starting transfers between devices  101 us (55%)
  waiting for transfers between devices  69.6 us (38%)
  other arithmetic  6.17 us (3%)
  local copies, waits for them, and re-layouts  6.16 us (3%)
    ppermute x15, waiting for transfers between devices, from_behind(): return lax.ppermute(block, axis, route)  54.2 us
    ppermute x12, starting transfers between devices, padded(): lax.ppermute(lax.slice_in_dim(block, block.shape[dim] - width, None, axis...  44.3 us
    ppermute x15, starting transfers between devices, from_behind(): return lax.ppermute(block, axis, route)  30.6 us
    ppermute x12, starting transfers between devices, padded(): lax.ppermute(lax.slice_in_dim(block, 0, width, axis=dim), axis, backward)  25.8 us
    ppermute x12, waiting for transfers between devices, padded(): lax.ppermute(lax.slice_in_dim(block, block.shape[dim] - width, None, axis...  11.4 us
    ppermute x12, waiting for transfers between devices, padded(): lax.ppermute(lax.slice_in_dim(block, 0, width, axis=dim), axis, backward)  3.95 us
  transfers between devices with their start and end apart: 39, of which 19 were waited for; matrix products, arithmetic and copies ran while one was open for 3% of the time, Pallas kernels for 0%

commit v1 on v0

v1 whole, which is shorter than its diff:
```python
import functools

import jax
import jax.numpy as jnp
from jax import lax
from jax.experimental import pallas as pl
from jax.experimental.pallas import tpu as pltpu
from jax.sharding import PartitionSpec as P

FINE = 4
GROUP = 4
LANES = 128
BLOCK = 4

diffusion = (0.05, 0.15, 0.4)
kappa_coupling = 0.1
time_step = 0.0125

VLO, VHI, BC, BLO, BHI, AC, ALO, AHI, LC, LLO, LHI, DC, DLO, DHI, SC, SLO, SHI, KINDS = range(18)
SENDS = 24


def shifted(x, by):
    sub, lanes = x.shape[-2:]
    lane = lax.broadcasted_iota(jnp.int32, (1, sub, lanes), 2)
    if by == 1:
        turned = pltpu.roll(x, lanes - 1, 2)
        return jnp.where(lane == lanes - 1, pltpu.roll(turned, sub - 1, 1), turned)
    turned = pltpu.roll(x, 1, 2)
    return jnp.where(lane == 0, pltpu.roll(turned, 1, 1), turned)


def step_rows(src, first, vel, vfirst, count, factor):
    vx, vy = vel[vfirst : vfirst + count, 0], vel[vfirst : vfirst + count, 1]
    u0 = src[first : first + count, 0]
    u1 = src[first : first + count, 1]
    ax = vx + kappa_coupling * u0
    ay = vy + kappa_coupling * u1
    axp, axn = jnp.maximum(ax, 0.0), jnp.minimum(ax, 0.0)
    ayp, ayn = jnp.maximum(ay, 0.0), jnp.minimum(ay, 0.0)
    out = []
    for c in range(3):
        u = (u0, u1)[c] if c < 2 else src[first : first + count, 2]
        n = src[first + 1 : first + 1 + count, c]
        s = src[first - 1 : first - 1 + count, c]
        e, w = shifted(u, 1), shifted(u, -1)
        adv = axp * (u - w) + axn * (e - u)
        adv = adv + ayp * (u - s) + ayn * (n - u)
        lap = n + s + e + w - 4.0 * u
        out.append(u + factor * (diffusion[c] * lap - adv))
    return out


def cycle(n_t, n_g, h, init_ref, ge_ref, vel_ref, cor_ref, rel_ref,
          ini, ge, vel, bufs, side, work, held, send_sem, recv_sem):
    t, g = lax.axis_index("tm"), lax.axis_index("gy")
    pos, cluster = lax.rem(t, GROUP), lax.div(t, GROUP)
    F = FINE
    level_one, coarsest = FINE * time_step, FINE * GROUP * time_step
    up, down = g < n_g - 1, g > 0
    last = GROUP - 1
    tiles = ge_ref.shape[-1] // LANES
    bbuf, lbuf, dbuf = bufs.at[0], bufs.at[1], bufs.at[2]
    abuf, sbuf = side.at[0], side.at[1]
    source, forcing, state, corr = held.at[0], held.at[1], held.at[2], held.at[3]

    def conj(*conditions):
        total = conditions[0]
        for other in conditions[1:]:
            total = jnp.logical_and(total, other)
        return total

    sends = []

    barrier = pltpu.get_barrier_semaphore()
    count = jnp.int32(0)
    for dt in (-GROUP, -1, 0, 1, GROUP):
        for dg in (-1, 0, 1):
            if dt == 0 and dg == 0:
                continue
            ok = conj(t + dt >= 0, t + dt < n_t, g + dg >= 0, g + dg < n_g)
            if abs(dt) == GROUP:
                ok = conj(ok, pos == last)
            @pl.when(ok)
            def _():
                pl.semaphore_signal(barrier, inc=1, device_id={"tm": t + dt, "gy": g + dg},
                                    device_id_type=pl.DeviceIdType.MESH)
            count = count + ok.astype(jnp.int32)

    def spread(src, index, dst, at):
        for c in range(src.shape[-3]):
            for k in range(tiles):
                rows = (src[index, c, :, k * LANES : (k + 1) * LANES] if index is not None
                        else src[c, :, k * LANES : (k + 1) * LANES])
                dst[at : at + h, c, k, :] = rows

    spread(vel_ref, 0, vel, F)
    spread(ge_ref, 0, ge, 0)
    @pl.when(jnp.logical_or(t == 0, t == last))
    def _():
        spread(init_ref, None, ini, 0)

    @pl.when(g == 0)
    def _():
        for b in (bbuf, lbuf, dbuf):
            b[0:F] = jnp.zeros((F,) + b.shape[1:], jnp.float32)
        for b in (abuf, sbuf):
            b[0:1] = jnp.zeros((1,) + b.shape[1:], jnp.float32)
        vel[0:F] = jnp.zeros((F,) + vel.shape[1:], jnp.float32)
    @pl.when(g == n_g - 1)
    def _():
        for b in (bbuf, lbuf, dbuf):
            b[F + h :] = jnp.zeros((F,) + b.shape[1:], jnp.float32)
        for b in (abuf, sbuf):
            b[1 + h :] = jnp.zeros((1,) + b.shape[1:], jnp.float32)
        vel[F + h :] = jnp.zeros((F,) + vel.shape[1:], jnp.float32)

    pl.semaphore_wait(barrier, count)

    def copy(src, dst, kind, dt, dg):
        return pltpu.make_async_remote_copy(
            src_ref=src, dst_ref=dst, send_sem=send_sem.at[len(sends)], recv_sem=recv_sem.at[kind],
            device_id={"tm": t + dt, "gy": g + dg}, device_id_type=pl.DeviceIdType.MESH)

    def edges(src, dst, kinds, dt, width, condition):
        for ok, rows, at, kind, dg in (
            (up, src.at[h - width : h], dst.at[0:width], kinds[0], 1),
            (down, src.at[0:width], dst.at[width + h : 2 * width + h], kinds[1], -1),
        ):
            move = copy(rows, at, kind, dt, dg)
            allowed = ok if condition is None else conj(ok, condition)
            pl.when(allowed)(move.start)
            sends.append((allowed, move))

    def whole(src, dst, kind, dt, width, condition):
        move = copy(src, dst.at[width : width + h], kind, dt, 0)
        pl.when(condition)(move.start)
        sends.append((condition, move))

    def arrived(dst, kinds, width, center=True, condition=None):
        def wait():
            if center:
                copy(held.at[0], dst.at[width : width + h], kinds[0], 0, 0).wait_recv()
            @pl.when(down)
            def _():
                copy(dst.at[0:width], dst.at[0:width], kinds[1], 0, 0).wait_recv()
            @pl.when(up)
            def _():
                copy(dst.at[0:width], dst.at[width + h : 2 * width + h], kinds[2], 0, 0).wait_recv()
        if condition is None:
            wait()
        else:
            pl.when(condition)(wait)

    center = vel.at[F : F + h]
    follows = t + 1 < n_t
    leaps = conj(pos == last, t + GROUP < n_t)
    edges(ge, bbuf, (BLO, BHI), 1, F, follows)
    whole(ge, bbuf, BC, 1, F, follows)
    edges(center, vel, (VLO, VHI), 0, F, None)
    edges(ini, bbuf, (BLO, BHI), 0, F, t == 0)
    edges(ini, abuf, (ALO, AHI), 0, 1, t == last)
    edges(ge, abuf, (ALO, AHI), GROUP, 1, leaps)
    whole(ge, abuf, AC, GROUP, 1, leaps)

    @pl.when(t == 0)
    def _():
        bbuf[F : F + h] = ini[...]
    @pl.when(t == last)
    def _():
        abuf[1 : 1 + h] = ini[...]

    def blocks(first, total):
        done = 0
        while done < total:
            size = min(BLOCK, total - done)
            yield first + done, size
            done += size

    def fine(src, final):
        here = src
        for section in range(F):
            halo = F - section - 1
            target = work.at[section % 2]
            for row, size in blocks(-halo, h + 2 * halo):
                new = step_rows(here, F + row, vel, F + row, size, time_step)
                if section == F - 1:
                    final(row, size, new)
                    continue
                for c in range(3):
                    value = new[c]
                    for i in range(size):
                        if row + i < 0:
                            target[F + row + i, c] = jnp.where(down, value[i], 0.0)
                        elif row + i >= h:
                            target[F + row + i, c] = jnp.where(up, value[i], 0.0)
                        else:
                            target[F + row + i, c] = value[i]
            here = target

    arrived(vel, (None, VLO, VHI), F, center=False)
    pl.when(t > 0)(lambda: copy(held.at[0], bbuf.at[F : F + h], BC, 0, 0).wait_recv())
    arrived(bbuf, (None, BLO, BHI), F, center=False)

    def keep_source(row, size, new):
        coarse = step_rows(bbuf, F + row, vel, F + row, size, level_one)
        for c in range(3):
            value = new[c] - coarse[c]
            source[row : row + size, c] = value
            state[row : row + size, c] = coarse[c] + value

    fine(bbuf, keep_source)

    def forward(src, dst, width, factor, added, target):
        for row, size in blocks(0, h):
            new = step_rows(src, width + row, vel, F + row, size, factor)
            for c in range(3):
                target[row : row + size, c] = new[c] + added[row : row + size, c]

    @pl.when(pos > 0)
    def _():
        arrived(lbuf, (LC, LLO, LHI), F)
        forward(lbuf, None, F, level_one, source, state)

    edges(state, lbuf, (LLO, LHI), 1, F, pos < last)
    whole(state, lbuf, LC, 1, F, pos < last)

    @pl.when(pos == last)
    def _():
        @pl.when(cluster > 0)
        def _():
            copy(held.at[0], abuf.at[1 : 1 + h], AC, 0, 0).wait_recv()
        arrived(abuf, (None, ALO, AHI), 1, center=False)
        for row, size in blocks(0, h):
            new = step_rows(abuf, 1 + row, vel, F + row, size, coarsest)
            for c in range(3):
                value = state[row : row + size, c] - new[c]
                forcing[row : row + size, c] = value
                corr[row : row + size, c] = new[c] + value
        @pl.when(cluster > 0)
        def _():
            arrived(sbuf, (SC, SLO, SHI), 1)
            forward(sbuf, None, 1, coarsest, forcing, corr)

    @pl.when(conj(pos < last, cluster == 0))
    def _():
        corr[...] = state[...]

    @pl.when(conj(pos < last, cluster > 0))
    def _():
        arrived(dbuf, (DC, DLO, DHI), F)
        forward(dbuf, None, F, level_one, source, corr)

    onward = conj(follows, jnp.logical_or(cluster > 0, pos == last))
    edges(corr, dbuf, (DLO, DHI), 1, F, onward)
    whole(corr, dbuf, DC, 1, F, onward)
    edges(corr, sbuf, (SLO, SHI), GROUP, 1, leaps)
    whole(corr, sbuf, SC, GROUP, 1, leaps)

    for c in range(3):
        for k in range(tiles):
            cor_ref[0, c, :, k * LANES : (k + 1) * LANES] = corr[:, c, k, :]

    arrived(dbuf, (DC, DLO, DHI), F, condition=conj(pos == last, cluster > 0))

    chosen = jnp.where(cluster > 0, 2, jnp.where(t > 0, 1, 0))

    def keep_relaxed(row, size, new):
        for c in range(3):
            source[row : row + size, c] = new[c]

    fine(bufs.at[chosen], keep_relaxed)
    for c in range(3):
        for k in range(tiles):
            rel_ref[0, c, :, k * LANES : (k + 1) * LANES] = source[:, c, k, :]

    for allowed, move in sends:
        pl.when(allowed)(move.wait_send)


def solution(mesh):
    n_t, n_g = mesh.shape["tm"], mesh.shape["gy"]

    def per_device(initial_state, guessed_ends, velocity):
        _, h, nx = initial_state.shape
        sub = nx // LANES
        F = FINE
        out = jax.ShapeDtypeStruct(guessed_ends.shape, jnp.float32)
        f32 = lambda *shape: pltpu.VMEM(shape + (sub, LANES), jnp.float32)
        whole = pl.BlockSpec(memory_space=pltpu.VMEM)
        return pl.pallas_call(
            functools.partial(cycle, n_t, n_g, h),
            out_shape=(out, out),
            in_specs=[whole] * 3,
            out_specs=(whole, whole),
            scratch_shapes=[
                f32(h, 3), f32(h, 3), f32(h + 2 * F, 2), f32(3, h + 2 * F, 3), f32(2, h + 2, 3),
                f32(2, h + 2 * F, 3), f32(4, h, 3),
                pltpu.SemaphoreType.DMA((SENDS,)), pltpu.SemaphoreType.DMA((KINDS,)),
            ],
            compiler_params=pltpu.CompilerParams(collective_id=0, has_side_effects=True),
            name="cycle",
        )(initial_state, guessed_ends, velocity)

    across = P("tm", None, "gy", None)
    return jax.shard_map(
        per_device, mesh=mesh, in_specs=(P(None, "gy", None), across, across),
        out_specs=(across, across), check_vma=False)
```

time: 185 us -> 42.5 us (0.23)
  the two profiles are of different devices: /device:TPU:20 before, /device:TPU:7 now
where the time goes in v1:
time: 42.5 us; the launch traced here: 42.3 us
  Pallas kernels  39.3 us (92%)
  local copies, waits for them, and re-layouts  2.34 us (6%)
  between operations  0.65 us (2%)
    pallas_call x1, Pallas kernels, per_device(): pl.pallas_call(functools.partial(cycle, n_t, n_g, h), out_shape=(out, out...  39.3 us
    unnamed x4, local copies, waits for them, and re-layouts  2.34 us

profile of v1, /device:TPU:7, one launch (start us, length us, event | category | flops | bytes accessed | tf_op | source)
XLA Modules:
  0.0 42.3 jit_solution(18084495501471515141)
XLA Ops:
  0.6 39.3 %cycle.1 = (f32[1,3,16,1024]{3,2,1,0:T(8,128)}, f32[1,3,16,1024]{3,2,1,0:T(8,128)}) custom-call(f32[3,16,1024]{2,1,0:T(8,128)} %init_ref.1, f32[1,3,16,1024]{3,2,1,0:T(8,128)} %ge_ref.1, f32[1,2,16,1024]{3,2,1,0:T(8,128)} %vel_ref.1), custom_call_target="tpu_custom_call" | custom-call | tf_op jit(solution)/shard_map/cycle/pallas_call | solution.py:291
  40.0 0.0 copy-start
  40.0 1.7 %copy.7 = f32[1,3,16,1024]{3,2,1,0:T(8,128)} copy(f32[1,3,16,1024]{3,2,1,0:T(8,128)} %get-tuple-element.4) | data formatting | bytes 393216
  41.6 0.0 copy-done
  41.6 0.7 %copy.8 = f32[1,3,16,1024]{3,2,1,0:T(8,128)} copy(f32[1,3,16,1024]{3,2,1,0:T(8,128)S(1)} %copy-done) | data formatting | bytes 393216
Async XLA Ops:
  40.0 1.7 %copy-start = (f32[1,3,16,1024]{3,2,1,0:T(8,128)S(1)}, f32[1,3,16,1024]{3,2,1,0:T(8,128)}, u32[]{:S(2)}) copy-start(f32[1,3,16,1024]{3,2,1,0:T(8,128)} %get-tuple-element.5) | copy-start | bytes 589828

commit v2 on v1

v2 whole, which is shorter than its diff:
```python
import functools

import jax
import jax.numpy as jnp
from jax import lax
from jax.experimental import pallas as pl
from jax.experimental.pallas import tpu as pltpu
from jax.sharding import PartitionSpec as P

FINE = 4
GROUP = 4
LANES = 128
BLOCK = 4

diffusion = (0.05, 0.15, 0.4)
kappa_coupling = 0.1
time_step = 0.0125

VLO, VHI, BC, BLO, BHI, AC, ALO, AHI, LC, LLO, LHI, DC, DLO, DHI, SC, SLO, SHI, KINDS = range(18)
SENDS = 40


def shifted(x, by):
    sub, lanes = x.shape[-2:]
    lane = lax.broadcasted_iota(jnp.int32, (1, sub, lanes), 2)
    if by == 1:
        turned = pltpu.roll(x, lanes - 1, 2)
        return jnp.where(lane == lanes - 1, pltpu.roll(turned, sub - 1, 1), turned)
    turned = pltpu.roll(x, 1, 2)
    return jnp.where(lane == 0, pltpu.roll(turned, 1, 1), turned)


def step_rows(src, first, vel, vfirst, count, factor):
    vx, vy = vel[vfirst : vfirst + count, 0], vel[vfirst : vfirst + count, 1]
    u0 = src[first : first + count, 0]
    u1 = src[first : first + count, 1]
    ax = vx + kappa_coupling * u0
    ay = vy + kappa_coupling * u1
    axp, axn = jnp.maximum(ax, 0.0), jnp.minimum(ax, 0.0)
    ayp, ayn = jnp.maximum(ay, 0.0), jnp.minimum(ay, 0.0)
    out = []
    for c in range(3):
        u = (u0, u1)[c] if c < 2 else src[first : first + count, 2]
        n = src[first + 1 : first + 1 + count, c]
        s = src[first - 1 : first - 1 + count, c]
        e, w = shifted(u, 1), shifted(u, -1)
        adv = axp * (u - w) + axn * (e - u)
        adv = adv + ayp * (u - s) + ayn * (n - u)
        lap = n + s + e + w - 4.0 * u
        out.append(u + factor * (diffusion[c] * lap - adv))
    return out


def cycle(n_t, n_g, h, init_ref, ge_ref, vel_ref, begin_ref, cor_ref, vel,
          ini, ge, bbuf, bufs, side, work, held, send_sem, recv_sem):
    t, g = lax.axis_index("tm"), lax.axis_index("gy")
    pos, cluster = lax.rem(t, GROUP), lax.div(t, GROUP)
    F = FINE
    level_one, coarsest = FINE * time_step, FINE * GROUP * time_step
    up, down = g < n_g - 1, g > 0
    last = GROUP - 1
    tiles = ge_ref.shape[-1] // LANES
    lbuf, dbuf = bufs.at[0], bufs.at[1]
    abuf, sbuf = side.at[0], side.at[1]
    source, forcing, state, corr = held.at[0], held.at[1], held.at[2], held.at[3]
    even = lax.rem(pos, 2) == 0
    H = F + 1

    def conj(*conditions):
        total = conditions[0]
        for other in conditions[1:]:
            total = jnp.logical_and(total, other)
        return total

    sends = []

    @pl.when(g == 0)
    def _():
        bbuf[0:H] = jnp.zeros((H,) + bbuf.shape[1:], jnp.float32)
        for b in (lbuf, dbuf):
            b[0:F] = jnp.zeros((F,) + b.shape[1:], jnp.float32)
        for b in (abuf, sbuf):
            b[0:1] = jnp.zeros((1,) + b.shape[1:], jnp.float32)
        vel[0:F] = jnp.zeros((F,) + vel.shape[1:], jnp.float32)
    @pl.when(g == n_g - 1)
    def _():
        bbuf[H + h :] = jnp.zeros((H,) + bbuf.shape[1:], jnp.float32)
        for b in (lbuf, dbuf):
            b[F + h :] = jnp.zeros((F,) + b.shape[1:], jnp.float32)
        for b in (abuf, sbuf):
            b[1 + h :] = jnp.zeros((1,) + b.shape[1:], jnp.float32)
        vel[F + h :] = jnp.zeros((F,) + vel.shape[1:], jnp.float32)

    barrier = pltpu.get_barrier_semaphore()
    count = jnp.int32(0)
    for dt in (-GROUP, -1, 0, 1, GROUP):
        for dg in (-1, 0, 1):
            if dt == 0 and dg == 0:
                continue
            ok = conj(t + dt >= 0, t + dt < n_t, g + dg >= 0, g + dg < n_g)
            if abs(dt) == GROUP:
                ok = conj(ok, pos == last)
            @pl.when(ok)
            def _():
                pl.semaphore_signal(barrier, inc=1, device_id={"tm": t + dt, "gy": g + dg},
                                    device_id_type=pl.DeviceIdType.MESH)
            count = count + ok.astype(jnp.int32)

    def spread(src, index, dst, at):
        for c in range(src.shape[-3]):
            for k in range(tiles):
                rows = (src[index, c, :, k * LANES : (k + 1) * LANES] if index is not None
                        else src[c, :, k * LANES : (k + 1) * LANES])
                dst[at : at + h, c, k, :] = rows

    spread(vel_ref, 0, vel, F)
    spread(ge_ref, 0, ge, 0)
    @pl.when(jnp.logical_or(t == 0, t == last))
    def _():
        spread(init_ref, None, ini, 0)

    pl.semaphore_wait(barrier, count)

    def copy(src, dst, kind, dt, dg):
        return pltpu.make_async_remote_copy(
            src_ref=src, dst_ref=dst, send_sem=send_sem.at[len(sends)], recv_sem=recv_sem.at[kind],
            device_id={"tm": t + dt, "gy": g + dg}, device_id_type=pl.DeviceIdType.MESH)

    def edges(src, dst, kinds, dt, width, condition):
        for ok, rows, at, kind, dg in (
            (up, src.at[h - width : h], dst.at[0:width], kinds[0], 1),
            (down, src.at[0:width], dst.at[width + h : 2 * width + h], kinds[1], -1),
        ):
            move = copy(rows, at, kind, dt, dg)
            allowed = ok if condition is None else conj(ok, condition)
            pl.when(allowed)(move.start)
            sends.append((allowed, move))

    def whole(src, dst, kind, dt, width, condition):
        move = copy(src, dst.at[width : width + h], kind, dt, 0)
        pl.when(condition)(move.start)
        sends.append((condition, move))

    def arrived(dst, kinds, width, center=True, condition=None):
        def wait():
            if center:
                copy(held.at[0, 1 : 1 + h], dst.at[width : width + h], kinds[0], 0, 0).wait_recv()
            @pl.when(down)
            def _():
                copy(dst.at[0:width], dst.at[0:width], kinds[1], 0, 0).wait_recv()
            @pl.when(up)
            def _():
                copy(dst.at[0:width], dst.at[width + h : 2 * width + h], kinds[2], 0, 0).wait_recv()
        if condition is None:
            wait()
        else:
            pl.when(condition)(wait)

    center = vel.at[F : F + h]
    follows = t + 1 < n_t
    leaps = conj(pos == last, t + GROUP < n_t)
    edges(ge, bbuf, (BLO, BHI), 1, H, follows)
    whole(ge, bbuf, BC, 1, H, follows)
    edges(center, vel, (VLO, VHI), 0, F, None)
    edges(ini, bbuf, (BLO, BHI), 0, H, t == 0)
    edges(ini, abuf, (ALO, AHI), 0, 1, t == last)
    edges(ge, abuf, (ALO, AHI), GROUP, 1, leaps)
    whole(ge, abuf, AC, GROUP, 1, leaps)

    @pl.when(t == 0)
    def _():
        bbuf[H : H + h] = ini[...]
    @pl.when(t == last)
    def _():
        abuf[1 : 1 + h] = ini[...]

    def blocks(first, total):
        done = 0
        while done < total:
            size = min(BLOCK, total - done)
            yield first + done, size
            done += size

    def put(target, at, row, size, new):
        for c in range(3):
            for i in range(size):
                value = new[c][i]
                if row + i < 0:
                    value = jnp.where(down, value, 0.0)
                elif row + i >= h:
                    value = jnp.where(up, value, 0.0)
                target[at + row + i, c] = value

    arrived(vel, (None, VLO, VHI), F, center=False)
    pl.when(t > 0)(lambda: copy(held.at[0, 1 : 1 + h], bbuf.at[H : H + h], BC, 0, 0).wait_recv())
    arrived(bbuf, (None, BLO, BHI), H, center=False)

    here = bbuf
    for section in range(F):
        halo = F - section
        for row, size in blocks(-halo, h + 2 * halo):
            new = step_rows(here, H + row, vel, F + row, size, time_step)
            if section < F - 1:
                put(work.at[section % 2], H, row, size, new)
                continue
            coarse = step_rows(bbuf, H + row, vel, F + row, size, level_one)
            value = [new[c] - coarse[c] for c in range(3)]
            put(source, 1, row, size, value)
            put(state, 1, row, size, [coarse[c] + value[c] for c in range(3)])
        here = work.at[section % 2]

    def forward(src, width, factor, added, target, extra):
        for row, size in blocks(-extra, h + 2 * extra):
            new = step_rows(src, width + row, vel, F + row, size, factor)
            put(target, 1, row, size,
                [new[c] + added[1 + row : 1 + row + size, c] for c in range(3)])

    def onto_next(src, dst, kinds, condition):
        center, lo, hi = kinds
        wide = conj(condition, even)
        move = copy(src, dst.at[F - 1 : F + 1 + h], center, 1, 0)
        pl.when(wide)(move.start)
        sends.append((wide, move))
        for ok, at, to, kind, dg in (
            (up, 1 + h - F, 0, lo, 1), (down, 2, F + h + 1, hi, -1),
        ):
            allowed = conj(wide, ok)
            move = copy(src.at[at : at + F - 1], dst.at[to : to + F - 1], kind, 1, dg)
            pl.when(allowed)(move.start)
            sends.append((allowed, move))
        narrow = conj(condition, jnp.logical_not(even))
        edges(src.at[1 : 1 + h], dst, (lo, hi), 1, F, narrow)
        whole(src.at[1 : 1 + h], dst, center, 1, F, narrow)

    def from_previous(dst, kinds, target):
        @pl.when(even)
        def _():
            arrived(dst, kinds, F)
            forward(dst, F, level_one, source, target, 1)
        @pl.when(jnp.logical_not(even))
        def _():
            copy(held.at[0], dst.at[F - 1 : F + 1 + h], kinds[0], 0, 0).wait_recv()
            forward(dst, F, level_one, source, target, 0)

    def outer_rows(dst, kinds, condition):
        @pl.when(conj(condition, down))
        def _():
            copy(held.at[0, 0 : F - 1], dst.at[0 : F - 1], kinds[1], 0, 0).wait_recv()
        @pl.when(conj(condition, up))
        def _():
            copy(held.at[0, 0 : F - 1], dst.at[F + h + 1 : 2 * F + h], kinds[2], 0, 0).wait_recv()

    odd = jnp.logical_not(even)
    L, D, S = (LC, LLO, LHI), (DC, DLO, DHI), (SC, SLO, SHI)
    pl.when(pos > 0)(lambda: from_previous(lbuf, L, state))
    onto_next(state, lbuf, L, pos < last)

    @pl.when(pos == last)
    def _():
        @pl.when(cluster > 0)
        def _():
            copy(held.at[0, 1 : 1 + h], abuf.at[1 : 1 + h], AC, 0, 0).wait_recv()
        arrived(abuf, (None, ALO, AHI), 1, center=False)
        for row, size in blocks(0, h):
            new = step_rows(abuf, 1 + row, vel, F + row, size, coarsest)
            value = [state[1 + row : 1 + row + size, c] - new[c] for c in range(3)]
            put(forcing, 1, row, size, value)
            put(corr, 1, row, size, [new[c] + value[c] for c in range(3)])
        @pl.when(cluster > 0)
        def _():
            arrived(sbuf, S, 1)
            forward(sbuf, 1, coarsest, forcing, corr, 0)

    @pl.when(conj(pos < last, cluster == 0))
    def _():
        corr[...] = state[...]

    pl.when(conj(pos < last, cluster > 0))(lambda: from_previous(dbuf, D, corr))

    onward = conj(follows, jnp.logical_or(cluster > 0, pos == last))
    onto_next(corr, dbuf, D, onward)
    edges(corr.at[1 : 1 + h], sbuf, (SLO, SHI), GROUP, 1, leaps)
    whole(corr.at[1 : 1 + h], sbuf, SC, GROUP, 1, leaps)
    cor_ref[...] = corr[1 : 1 + h]

    @pl.when(conj(pos == last, cluster > 0))
    def _():
        copy(held.at[0], dbuf.at[F - 1 : F + 1 + h], DC, 0, 0).wait_recv()
    outer_rows(lbuf, L, odd)
    outer_rows(dbuf, D, conj(odd, cluster > 0))

    @pl.when(t == 0)
    def _():
        begin_ref[...] = bbuf[1 : 1 + h + 2 * F]
    @pl.when(t > 0)
    def _():
        begin_ref[...] = bufs[jnp.where(cluster > 0, 1, 0)]

    for allowed, move in sends:
        pl.when(allowed)(move.wait_send)


def relax(n_g, h, begin, cor, vel, cor_ref, rel_ref, work):
    g = lax.axis_index("gy")
    up, down = g < n_g - 1, g > 0
    F = FINE
    tiles = cor_ref.shape[-1] // LANES
    for c in range(3):
        for k in range(tiles):
            cor_ref[0, c, :, k * LANES : (k + 1) * LANES] = cor[:, c, k, :]
    here = begin
    for section in range(F):
        halo = F - section - 1
        target = work.at[section % 2]
        row = -halo
        while row < h + halo:
            size = min(BLOCK, h + halo - row)
            new = step_rows(here, F + row, vel, F + row, size, time_step)
            for c in range(3):
                for i in range(size):
                    value = new[c][i]
                    if row + i < 0:
                        value = jnp.where(down, value, 0.0)
                    elif row + i >= h:
                        value = jnp.where(up, value, 0.0)
                    target[F + row + i, c] = value
            row += size
        here = target
    for c in range(3):
        for k in range(tiles):
            rel_ref[0, c, :, k * LANES : (k + 1) * LANES] = here[F : F + h, c, k, :]


def solution(mesh):
    n_t, n_g = mesh.shape["tm"], mesh.shape["gy"]

    def per_device(initial_state, guessed_ends, velocity):
        _, h, nx = initial_state.shape
        sub = nx // LANES
        F = FINE
        out = jax.ShapeDtypeStruct(guessed_ends.shape, jnp.float32)
        f32 = lambda *shape: pltpu.VMEM(shape + (sub, LANES), jnp.float32)
        whole = pl.BlockSpec(memory_space=pltpu.VMEM)
        shape = lambda *dims: jax.ShapeDtypeStruct(dims + (sub, LANES), jnp.float32)
        begin, corrected, flow = pl.pallas_call(
            functools.partial(cycle, n_t, n_g, h),
            out_shape=(shape(h + 2 * F, 3), shape(h, 3), shape(h + 2 * F, 2)),
            in_specs=[whole] * 3,
            out_specs=(whole,) * 3,
            scratch_shapes=[
                f32(h, 3), f32(h, 3), f32(h + 2 * F + 2, 3), f32(2, h + 2 * F, 3),
                f32(2, h + 2, 3), f32(2, h + 2 * F + 2, 3), f32(4, h + 2, 3),
                pltpu.SemaphoreType.DMA((SENDS,)), pltpu.SemaphoreType.DMA((KINDS,)),
            ],
            compiler_params=pltpu.CompilerParams(
                collective_id=0, has_side_effects=True, vmem_limit_bytes=16 * 2**20),
            name="cycle",
        )(initial_state, guessed_ends, velocity)
        return pl.pallas_call(
            functools.partial(relax, n_g, h),
            out_shape=(out, out),
            in_specs=[whole] * 3,
            out_specs=(whole, whole),
            scratch_shapes=[f32(2, h + 2 * F, 3)],
            compiler_params=pltpu.CompilerParams(vmem_limit_bytes=16 * 2**20),
            name="relax",
        )(begin, corrected, flow)

    across = P("tm", None, "gy", None)
    return jax.shard_map(
        per_device, mesh=mesh, in_specs=(P(None, "gy", None), across, across),
        out_specs=(across, across), check_vma=False)
```

time: 42.5 us -> 37.7 us (0.89)
  Pallas kernels: 39.3 us -> 34.2 us
    pallas_call x1 -> x2, Pallas kernels: 39.3 us -> 34.2 us  [the longest x1 32.3 us: per_device(): pl.pallas_call(functools.partial(cycle, n_t, n_g, h), out_shape=(shape(h...]
    unnamed x4 -> x6, local copies, waits for them, and re-layouts: 2.34 us -> 2.75 us
where the time goes in v2:
time: 37.7 us; the launch traced here: 37.6 us
  Pallas kernels  34.2 us (91%)
  local copies, waits for them, and re-layouts  2.75 us (7%)
  between operations  0.65 us (2%)
    pallas_call x1, Pallas kernels, per_device(): pl.pallas_call(functools.partial(cycle, n_t, n_g, h), out_shape=(shape(h...  32.3 us
    unnamed x6, local copies, waits for them, and re-layouts  2.75 us
    pallas_call x1, Pallas kernels, per_device(): pl.pallas_call(functools.partial(relax, n_g, h), out_shape=(out, out), in...  1.86 us

profile of v2, /device:TPU:7, one launch (start us, length us, event | category | flops | bytes accessed | tf_op | source)
XLA Modules:
  0.0 37.6 jit_solution(1736701143988690201)
XLA Ops:
  0.6 0.0 copy-start
  0.6 0.9 %copy-done = f32[3,16,1024]{2,1,0:T(8,128)S(1)} copy-done((f32[3,16,1024]{2,1,0:T(8,128)S(1)}, f32[3,16,1024]{2,1,0:T(8,128)}, u32[]{:S(2)}) %copy-start) | copy-done | bytes 196632
  1.6 0.0 copy-start.1
  1.6 0.9 %copy-done.1 = f32[1,3,16,1024]{3,2,1,0:T(8,128)S(1)} copy-done((f32[1,3,16,1024]{3,2,1,0:T(8,128)S(1)}, f32[1,3,16,1024]{3,2,1,0:T(8,128)}, u32[]{:S(2)}) %copy-start.1) | copy-done | bytes 196632
  2.5 0.0 copy-start.2
  2.5 0.9 %copy-done.2 = f32[1,2,16,1024]{3,2,1,0:T(8,128)S(1)} copy-done((f32[1,2,16,1024]{3,2,1,0:T(8,128)S(1)}, f32[1,2,16,1024]{3,2,1,0:T(8,128)}, u32[]{:S(2)}) %copy-start.2) | copy-done | bytes 131096
  3.4 32.3 %cycle.1 = (f32[24,3,8,128]{3,2,1,0:T(8,128)S(1)}, f32[16,3,8,128]{3,2,1,0:T(8,128)S(1)}, f32[24,2,8,128]{3,2,1,0:T(8,128)S(1)}) custom-call(f32[3,16,1024]{2,1,0:T(8,128)S(1)} %copy-done, f32[1,3,16,1024]{3,2,1,0:T(8,128)S(1)} %copy-done.1, f32[1,2,16,1024]{3,2,1,0:T(8,128)S(1)} %copy-done.2), custom_call_target="tpu_custom_call" | custom-call | tf_op jit(solution)/shard_map/cycle/pallas_call | solution.py:345
  35.7 1.9 %relax.1 = (f32[1,3,16,1024]{3,2,1,0:T(8,128)}, f32[1,3,16,1024]{3,2,1,0:T(8,128)}) custom-call(f32[24,3,8,128]{3,2,1,0:T(8,128)S(1)} %get-tuple-element.5.begin, f32[16,3,8,128]{3,2,1,0:T(8,128)S(1)} %get-tuple-element.6.cor, f32[24,2,8,128]{3,2,1,0:T(8,128)S(1)} %get-tuple-element.7.vel), custom_call_target="tpu_custom_call" | custom-call | tf_op jit(solution)/shard_map/relax/pallas_call | solution.py:359
Async XLA Ops:
  0.6 0.9 %copy-start = (f32[3,16,1024]{2,1,0:T(8,128)S(1)}, f32[3,16,1024]{2,1,0:T(8,128)}, u32[]{:S(2)}) copy-start(f32[3,16,1024]{2,1,0:T(8,128)} %init_ref.1) | copy-start | bytes 589828
  1.6 0.9 %copy-start.1 = (f32[1,3,16,1024]{3,2,1,0:T(8,128)S(1)}, f32[1,3,16,1024]{3,2,1,0:T(8,128)}, u32[]{:S(2)}) copy-start(f32[1,3,16,1024]{3,2,1,0:T(8,128)} %ge_ref.1) | copy-start | bytes 589828
  2.5 0.9 %copy-start.2 = (f32[1,2,16,1024]{3,2,1,0:T(8,128)S(1)}, f32[1,2,16,1024]{3,2,1,0:T(8,128)}, u32[]{:S(2)}) copy-start(f32[1,2,16,1024]{3,2,1,0:T(8,128)} %vel_ref.1) | copy-start | bytes 393220

commit v3 on v2

--- a/solution.py
+++ b/solution.py
@@ -16,7 +16,7 @@
 kappa_coupling = 0.1
 time_step = 0.0125
 
-VLO, VHI, BC, BLO, BHI, AC, ALO, AHI, LC, LLO, LHI, DC, DLO, DHI, SC, SLO, SHI, KINDS = range(18)
+VLO, VHI, BC, BLO, BHI, AC, ALO, AHI, LC, LLO, LHI, DC, DLO, DHI, SC, SLO, SHI, LOL, LOH, DOL, DOH, KINDS = range(22)
 SENDS = 40
 
 
@@ -216,7 +216,7 @@
                 [new[c] + added[1 + row : 1 + row + size, c] for c in range(3)])
 
     def onto_next(src, dst, kinds, condition):
-        center, lo, hi = kinds
+        center, lo, hi, outer_lo, outer_hi = kinds
         wide = conj(condition, even)
         move = copy(src, dst.at[F - 1 : F + 1 + h], center, 1, 0)
         pl.when(wide)(move.start)
@@ -229,32 +229,37 @@
             pl.when(allowed)(move.start)
             sends.append((allowed, move))
         narrow = conj(condition, jnp.logical_not(even))
-        edges(src.at[1 : 1 + h], dst, (lo, hi), 1, F, narrow)
+        edges(src.at[1 : 1 + h], dst.at[F - 2 : F + h + 2], (lo, hi), 1, 2, narrow)
         whole(src.at[1 : 1 + h], dst, center, 1, F, narrow)
+        for ok, at, to, kind, dg in (
+            (up, 1 + h - F, 0, outer_lo, 1), (down, 3, F + h + 2, outer_hi, -1),
+        ):
+            allowed = conj(narrow, ok)
+            move = copy(src.at[at : at + F - 2], dst.at[to : to + F - 2], kind, 1, dg)
+            pl.when(allowed)(move.start)
+            sends.append((allowed, move))
 
     def from_previous(dst, kinds, target):
         @pl.when(even)
         def _():
-            arrived(dst, kinds, F)
+            copy(held.at[0, 1 : 1 + h], dst.at[F : F + h], kinds[0], 0, 0).wait_recv()
+            arrived(dst.at[F - 2 : F + h + 2], kinds, 2, center=False)
             forward(dst, F, level_one, source, target, 1)
         @pl.when(jnp.logical_not(even))
         def _():
             copy(held.at[0], dst.at[F - 1 : F + 1 + h], kinds[0], 0, 0).wait_recv()
             forward(dst, F, level_one, source, target, 0)
 
-    def outer_rows(dst, kinds, condition):
+    def outer_rows(dst, lo, hi, width, condition):
         @pl.when(conj(condition, down))
         def _():
-            copy(held.at[0, 0 : F - 1], dst.at[0 : F - 1], kinds[1], 0, 0).wait_recv()
+            copy(held.at[0, 0:width], dst.at[0:width], lo, 0, 0).wait_recv()
         @pl.when(conj(condition, up))
         def _():
-            copy(held.at[0, 0 : F - 1], dst.at[F + h + 1 : 2 * F + h], kinds[2], 0, 0).wait_recv()
+            copy(held.at[0, 0:width], dst.at[2 * F + h - width :], hi, 0, 0).wait_recv()
 
     odd = jnp.logical_not(even)
-    L, D, S = (LC, LLO, LHI), (DC, DLO, DHI), (SC, SLO, SHI)
-    pl.when(pos > 0)(lambda: from_previous(lbuf, L, state))
-    onto_next(state, lbuf, L, pos < last)
-
+    L, D, S = (LC, LLO, LHI, LOL, LOH), (DC, DLO, DHI, DOL, DOH), (SC, SLO, SHI)
     @pl.when(pos == last)
     def _():
         @pl.when(cluster > 0)
@@ -262,10 +267,19 @@
             copy(held.at[0, 1 : 1 + h], abuf.at[1 : 1 + h], AC, 0, 0).wait_recv()
         arrived(abuf, (None, ALO, AHI), 1, center=False)
         for row, size in blocks(0, h):
-            new = step_rows(abuf, 1 + row, vel, F + row, size, coarsest)
-            value = [state[1 + row : 1 + row + size, c] - new[c] for c in range(3)]
-            put(forcing, 1, row, size, value)
-            put(corr, 1, row, size, [new[c] + value[c] for c in range(3)])
+            put(corr, 1, row, size, step_rows(abuf, 1 + row, vel, F + row, size, coarsest))
+
+    pl.when(pos > 0)(lambda: from_previous(lbuf, L, state))
+    onto_next(state, lbuf, L, pos < last)
+
+    @pl.when(pos == last)
+    def _():
+        for row, size in blocks(1, h):
+            for c in range(3):
+                begun = corr[row : row + size, c]
+                value = state[row : row + size, c] - begun
+                forcing[row : row + size, c] = value
+                corr[row : row + size, c] = begun + value
         @pl.when(cluster > 0)
         def _():
             arrived(sbuf, S, 1)
@@ -286,8 +300,10 @@
     @pl.when(conj(pos == last, cluster > 0))
     def _():
         copy(held.at[0], dbuf.at[F - 1 : F + 1 + h], DC, 0, 0).wait_recv()
-    outer_rows(lbuf, L, odd)
-    outer_rows(dbuf, D, conj(odd, cluster > 0))
+    outer_rows(lbuf, LLO, LHI, F - 1, odd)
+    outer_rows(dbuf, DLO, DHI, F - 1, conj(odd, cluster > 0))
+    outer_rows(lbuf, LOL, LOH, F - 2, conj(even, pos > 0))
+    outer_rows(dbuf, DOL, DOH, F - 2, conj(even, cluster > 0))
 
     @pl.when(t == 0)
     def _():

time: 37.7 us -> 37.6 us (level)
  no operation moved by 1% of the time
where the time goes in v3:
time: 37.6 us; the launch traced here: 37.4 us
  Pallas kernels  34 us (90%)
  local copies, waits for them, and re-layouts  2.75 us (7%)
  between operations  0.65 us (2%)
    pallas_call x1, Pallas kernels, per_device(): pl.pallas_call(functools.partial(cycle, n_t, n_g, h), out_shape=(shape(h...  32.2 us
    unnamed x6, local copies, waits for them, and re-layouts  2.75 us
    pallas_call x1, Pallas kernels, per_device(): pl.pallas_call(functools.partial(relax, n_g, h), out_shape=(out, out), in...  1.86 us

profile of v3, /device:TPU:7, one launch (start us, length us, event | category | flops | bytes accessed | tf_op | source)
XLA Modules:
  0.0 37.4 jit_solution(1549698487537608701)
XLA Ops:
  0.6 0.0 copy-start
  0.6 0.9 %copy-done = f32[3,16,1024]{2,1,0:T(8,128)S(1)} copy-done((f32[3,16,1024]{2,1,0:T(8,128)S(1)}, f32[3,16,1024]{2,1,0:T(8,128)}, u32[]{:S(2)}) %copy-start) | copy-done | bytes 196632
  1.6 0.0 copy-start.1
  1.6 0.9 %copy-done.1 = f32[1,3,16,1024]{3,2,1,0:T(8,128)S(1)} copy-done((f32[1,3,16,1024]{3,2,1,0:T(8,128)S(1)}, f32[1,3,16,1024]{3,2,1,0:T(8,128)}, u32[]{:S(2)}) %copy-start.1) | copy-done | bytes 196632
  2.5 0.0 copy-start.2
  2.5 0.9 %copy-done.2 = f32[1,2,16,1024]{3,2,1,0:T(8,128)S(1)} copy-done((f32[1,2,16,1024]{3,2,1,0:T(8,128)S(1)}, f32[1,2,16,1024]{3,2,1,0:T(8,128)}, u32[]{:S(2)}) %copy-start.2) | copy-done | bytes 131096
  3.4 32.2 %cycle.1 = (f32[24,3,8,128]{3,2,1,0:T(8,128)S(1)}, f32[16,3,8,128]{3,2,1,0:T(8,128)S(1)}, f32[24,2,8,128]{3,2,1,0:T(8,128)S(1)}) custom-call(f32[3,16,1024]{2,1,0:T(8,128)S(1)} %copy-done, f32[1,3,16,1024]{3,2,1,0:T(8,128)S(1)} %copy-done.1, f32[1,2,16,1024]{3,2,1,0:T(8,128)S(1)} %copy-done.2), custom_call_target="tpu_custom_call" | custom-call | tf_op jit(solution)/shard_map/cycle/pallas_call | solution.py:361
  35.6 1.9 %relax.1 = (f32[1,3,16,1024]{3,2,1,0:T(8,128)}, f32[1,3,16,1024]{3,2,1,0:T(8,128)}) custom-call(f32[24,3,8,128]{3,2,1,0:T(8,128)S(1)} %get-tuple-element.5.begin, f32[16,3,8,128]{3,2,1,0:T(8,128)S(1)} %get-tuple-element.6.cor, f32[24,2,8,128]{3,2,1,0:T(8,128)S(1)} %get-tuple-element.7.vel), custom_call_target="tpu_custom_call" | custom-call | tf_op jit(solution)/shard_map/relax/pallas_call | solution.py:375
Async XLA Ops:
  0.6 0.9 %copy-start = (f32[3,16,1024]{2,1,0:T(8,128)S(1)}, f32[3,16,1024]{2,1,0:T(8,128)}, u32[]{:S(2)}) copy-start(f32[3,16,1024]{2,1,0:T(8,128)} %init_ref.1) | copy-start | bytes 589828
  1.6 0.9 %copy-start.1 = (f32[1,3,16,1024]{3,2,1,0:T(8,128)S(1)}, f32[1,3,16,1024]{3,2,1,0:T(8,128)}, u32[]{:S(2)}) copy-start(f32[1,3,16,1024]{3,2,1,0:T(8,128)} %ge_ref.1) | copy-start | bytes 589828
  2.5 0.9 %copy-start.2 = (f32[1,2,16,1024]{3,2,1,0:T(8,128)S(1)}, f32[1,2,16,1024]{3,2,1,0:T(8,128)}, u32[]{:S(2)}) copy-start(f32[1,2,16,1024]{3,2,1,0:T(8,128)} %vel_ref.1) | copy-start | bytes 393220
